TPU v7x, 32 devices: a whole 2x2x4 slice. The times are simulated.
32 devices in a mesh: row: 8 (over z, core), col: 4 (over y, x).
Axes of the slice: x: 2, y: 2, z: 4, core: 2. Of those that a mesh axis runs over, the one named last changes fastest.
Arguments:
- velocity: float32 [1, 3, 64, 64, 256], P(None, None, 'row', 'col'), may hold values from -6 to 6
- tendency: float32 [1, 3, 64, 64, 256], P(None, None, 'row', 'col'), may hold values from -6 to 6
- step_size: float32 [1], replicated, may hold values from 0.1 to 0.6
- lift_weight: float32 [32, 3], replicated, may hold values from -3.5 to 3.5
- lift_bias: float32 [32], replicated, may hold values from -3 to 3
- spectral_weight: bfloat16 [2, 32, 32, 32, 1024], P(None, 'row', 'col'), may hold values from -6 to 6
- local_weight: float32 [32, 32], replicated, may hold values from -1 to 1
- local_bias: float32 [32], replicated, may hold values from -3 to 3
Outputs:
- features: bfloat16 [1, 32, 64, 64, 256], P(None, None, 'row', 'col')
All inputs are finite; a program needn't handle non-finite values.
Results may differ from a plain program's by a relative error of at most 0.001.
Values sent between devices are 32-bit elements; how exact they have to be, the bound alone decides.
A program may use at most 64 MiB of HBM per device.

v0:
```python
import functools
import math

import jax
import jax.numpy as jnp
import numpy as np
from jax import lax
from jax.experimental import pallas as pl
from jax.experimental.pallas import tpu as pltpu
from jax.sharding import PartitionSpec as P

KX = 32
KY = 32
KZ = 32
HIGHEST = lax.Precision.HIGHEST
F32 = jnp.float32
BF16 = jnp.bfloat16


def waves(count):
    index = np.arange(count)
    return np.where(index < count // 2, index, index - count)


def trig(wave, length):
    angle = ((wave[:, None] * np.arange(length)[None, :]) % length) * (2.0 * math.pi / length)
    return np.cos(angle), np.sin(angle)


def np_halves(table):
    table = np.asarray(table, np.float32)
    high = table.astype(jnp.bfloat16)
    low = (table - high.astype(np.float32)).astype(jnp.bfloat16)
    return high, low


def split(x):
    high = x.astype(BF16)
    return high, (x - high.astype(F32)).astype(BF16)


def dot(a, b):
    return jnp.dot(a, b, preferred_element_type=F32)


def mix_kernel(kyl, kzl, scale, u_ref, wl_ref, xf_ref, selc_ref, sels_ref, flag_ref, xb_ref, out_ref, m_ref):
    sources, rows, wide = u_ref.shape
    a = rows // kyl
    cos_parts, sin_parts = [], []
    for l in range(kyl):
        u = u_ref[:, l * a:(l + 1) * a, :].reshape(sources * a, wide)
        q = jnp.dot(xf_ref[...], u, precision=HIGHEST, preferred_element_type=F32) * scale
        cos_parts.append(q[:KX])
        sin_parts.append(q[KX:])
    ch, cl = split(jnp.concatenate(cos_parts, 0))
    sh, sl = split(jnp.concatenate(sin_parts, 0))
    selc, sels = selc_ref[...], sels_ref[...]
    amp = dot(ch, selc) + dot(cl, selc) + dot(sh, sels) + dot(sl, sels)
    lane = lax.broadcasted_iota(jnp.int32, (KX, 128), 1)
    row = lax.broadcasted_iota(jnp.int32, (KX, 128), 0)
    quarter = lane // 32
    for group in range(kyl * kzl // 4):
        packed_r = packed_i = None
        for q in range(4):
            l, k = divmod(group * 4 + q, kzl)
            ar = amp[l * KX:(l + 1) * KX, k * 256:k * 256 + 128]
            ai = amp[l * KX:(l + 1) * KX, k * 256 + 128:k * 256 + 256]
            if l == 0 and k == 0:
                ar = ar + jnp.where(row == 0, flag_ref[...], 0.0)
            at = pl.ds((l * kzl + k) * KX, KX)
            wr = wl_ref[0, at, :128] + wl_ref[0, at, 128:]
            wi = wl_ref[1, at, :128] + wl_ref[1, at, 128:]
            pr = wr * ar - wi * ai
            pi = wr * ai + wi * ar
            pr = pr + pltpu.roll(pr, 64, 1)
            pi = pi + pltpu.roll(pi, 64, 1)
            pr = pr + pltpu.roll(pr, 32, 1)
            pi = pi + pltpu.roll(pi, 32, 1)
            packed_r = pr if q == 0 else jnp.where(quarter == q, pr, packed_r)
            packed_i = pi if q == 0 else jnp.where(quarter == q, pi, packed_i)
        cols = slice(group * 128, (group + 1) * 128)
        m = jnp.concatenate([packed_r, packed_i], 0)
        mh, ml = split(m)
        m_ref[0:2 * KX, cols] = mh
        m_ref[2 * KX:4 * KX, cols] = ml
        m_ref[4 * KX:6 * KX, cols] = mh
    back = dot(xb_ref[...], m_ref[...])
    out_ref[...] = back.reshape(out_ref.shape)


def y_back_kernel(kyl, d_ref, yh_ref, yl_ref, out_ref, lhs_ref):
    total = d_ref.shape[0]
    ko = d_ref.shape[1] // kyl
    count, halves_v, _, cells = out_ref.shape
    pairs = yh_ref.shape[1]
    a = total // pairs
    for l in range(kyl):
        t = jnp.transpose(d_ref[:, l * ko:(l + 1) * ko])
        th, tl = split(t)
        lhs_ref[:, l * total:(l + 1) * total] = th
        lhs_ref[:, (kyl + l) * total:(kyl + l + 1) * total] = tl
        lhs_ref[:, (2 * kyl + l) * total:(2 * kyl + l + 1) * total] = th
    width = halves_v * cells
    b = cells // a
    xr = lax.broadcasted_iota(jnp.int32, (pairs, a, width), 1)
    xl = (lax.broadcasted_iota(jnp.int32, (pairs, a, width), 2) // b) % a
    same = xr == xl

    def expand(table):
        full = jnp.where(same, table.astype(F32)[:, None, :], 0.0)
        return full.reshape(total, width).astype(BF16)

    for d in range(count):
        cols = slice(d * width, (d + 1) * width)
        high = [expand(yh_ref[l, :, cols]) for l in range(kyl)]
        low = [expand(yl_ref[l, :, cols]) for l in range(kyl)]
        rhs = jnp.concatenate(high + high + low, 0)
        acc = dot(lhs_ref[...], rhs)
        for v in range(halves_v):
            out_ref[d, v] = acc[:, v * cells:(v + 1) * cells]


def z_back_kernel(channels, block, d_ref, vel_ref, tend_ref, step_ref, comb_ref, off_ref, tz_ref, out_ref, adv_ref):
    first = pl.program_id(0)
    depth = d_ref.shape[0] // channels

    @pl.when(first == 0)
    def _():
        adv_ref[...] = vel_ref[...] + step_ref[0] * tend_ref[...]

    for i in range(block):
        o = first * block + i
        high, low = split(d_ref[pl.ds(o, depth, stride=channels), :])
        lhs = jnp.concatenate([high, low, high], 0)
        spectral = lax.dot_general(lhs, tz_ref[...], (((0,), (0,)), ((), ())), preferred_element_type=F32)
        x = spectral + off_ref[o]
        for j in range(adv_ref.shape[0]):
            x = x + comb_ref[o, j] * adv_ref[j]
        inner = x * (0.7978845608028654 + 0.035677408136300125 * (x * x))
        half = 0.5 * x
        out_ref[i] = (half + half * jnp.tanh(inner)).astype(BF16)


def per_device(
    velocity, tendency, step_size, lift_weight, lift_bias, spectral_weight, local_weight, local_bias
):
    samples, width_in, a, b, nz = velocity.shape
    channels = lift_weight.shape[0]
    rows, cols = lax.axis_size("row"), lax.axis_size("col")
    full_x, full_y = a * rows, b * cols
    kzl, kyl = KZ // cols, KY // rows
    modes = kyl * kzl * KX
    cells = a * b
    vmem = pl.BlockSpec(memory_space=pltpu.VMEM)
    smem = pl.BlockSpec(memory_space=pltpu.SMEM)
    big = pltpu.CompilerParams(vmem_limit_bytes=48 * 1024 * 1024)

    lift4 = jnp.concatenate([lift_weight, lift_bias[:, None]], 1)
    group = width_in + 1
    eye = jnp.eye(channels, dtype=F32)
    lift_lanes = jnp.repeat(lift4, channels, axis=1)
    lift_full = jnp.tile(lift_lanes, (channels, 1))
    own = jnp.tile(jnp.repeat(eye, channels, axis=0), (1, group))
    masked = lift_full * own
    high = lax.reduce_precision(masked, 8, 7)
    lh, ll = high.astype(BF16), (masked - high).astype(BF16)
    stored = spectral_weight.reshape(2 * modes, channels * channels)
    lifted_weight = dot(stored, jnp.concatenate([lh, ll], 1)).reshape(2, modes, 2 * group * channels)

    zc, zs = trig(np.arange(KZ), nz)
    zf = np.stack([zc, -zs], 0).reshape(2, cols, kzl, nz).transpose(1, 0, 2, 3).reshape(2 * KZ, nz)
    yc, ys = trig(waves(KY), full_y)
    xc, xs = trig(waves(KX), full_x)
    xf = np.concatenate([xc, xs], 0).astype(np.float32)
    selc = np.zeros((2, width_in, kzl, kzl, 2, group, channels), np.float32)
    sels = np.zeros_like(selc)
    for j in range(width_in):
        for k in range(kzl):
            selc[0, j, k, k, 0, j] = 1
            selc[1, j, k, k, 1, j] = 1
            sels[1, j, k, k, 0, j] = 1
            sels[0, j, k, k, 1, j] = -1
    wide = 2 * width_in * kzl
    selc = selc.reshape(wide, -1)
    sels = sels.reshape(wide, -1)
    xb = np.stack([np.stack([xc, -xs], 0), np.stack([xs, xc], 0)], 0)
    xb = xb.reshape(2, 2, KX, rows, a).transpose(3, 0, 4, 1, 2).reshape(rows * 2 * a, 2 * KX)
    xbh, xbl = np_halves(xb)
    xb3 = np.concatenate([xbh, xbh, xbl], 1)
    yb = np.stack([np.stack([yc, ys], 0), np.stack([-ys, yc], 0)], 0)
    yb = yb.reshape(2, 2, rows, kyl, cols, b).transpose(3, 2, 0, 4, 1, 5)
    yb = np.broadcast_to(yb[:, :, :, :, :, None, :], (kyl, rows, 2, cols, 2, a, b)).reshape(kyl, rows * 2, cols * 2 * cells)
    ybh, ybl = np_halves(yb)
    twice = np.where(np.arange(KZ) == 0, 1.0, 2.0)[:, None]
    zb = np.stack([twice * zc, -twice * zs], 0).reshape(2, cols, kzl, nz).transpose(1, 0, 2, 3).reshape(2 * KZ, nz)
    zbh, zbl = np_halves(zb)
    zb3 = np.concatenate([zbh, zbh, zbl], 0)
    yf = np.stack([yc, ys], 0).reshape(2, rows, kyl, 1, cols, 1, b)
    yf = (yf * np.eye(a).reshape(1, 1, 1, a, 1, a, 1)).reshape(2, rows * kyl * a, cols, cells)

    combined = jnp.dot(local_weight, lift_weight, precision=HIGHEST)
    offset = jnp.dot(local_weight, lift_bias, precision=HIGHEST) + local_bias
    origin = (lax.axis_index("row") == 0) & (lax.axis_index("col") == 0)
    last = np.arange(group * channels)[None, :] >= width_in * channels
    flag = jnp.where(jnp.asarray(last) & origin, 1.0, 0.0).astype(F32)

    results = []
    for sample in range(samples):
        vel = velocity[sample].reshape(width_in * cells, nz)
        tend = tendency[sample].reshape(width_in * cells, nz)
        step = step_size[sample]
        advanced = vel + step * tend
        z_modes = lax.dot_general(jnp.asarray(zf, F32), advanced, (((1,), (1,)), ((), ())), precision=HIGHEST)
        arrived = lax.all_to_all(z_modes.reshape(cols, 2 * kzl, width_in * cells), "col", 0, 0, tiled=True)
        arrived = arrived.reshape(cols, 2, kzl, width_in, cells)
        by_y = jnp.einsum("pgsn,srkjn->pgrjk", jnp.asarray(yf, F32), arrived, precision=HIGHEST)
        real = by_y[0, :, 0] + by_y[1, :, 1]
        imag = by_y[0, :, 1] - by_y[1, :, 0]
        by_y = jnp.stack([real, imag], 1).reshape(rows, kyl * a, wide)
        pencils_x = lax.all_to_all(by_y, "row", 0, 0, tiled=True)
        cells_x = pl.pallas_call(
            functools.partial(mix_kernel, kyl, kzl, 1.0 / (full_x * full_y * nz)),
            out_shape=jax.ShapeDtypeStruct((rows, 2 * a, kyl * kzl * channels), F32),
            in_specs=[vmem] * 7,
            out_specs=vmem,
            scratch_shapes=[pltpu.VMEM((6 * KX, kyl * kzl * channels), BF16)],
            compiler_params=big,
        )(pencils_x, lifted_weight, jnp.asarray(xf), jnp.asarray(selc, BF16), jnp.asarray(sels, BF16), flag, jnp.asarray(xb3))
        by_cells = lax.all_to_all(cells_x, "row", 0, 0, tiled=True)
        by_cells = by_cells.reshape(rows * 2 * a, kyl * kzl * channels)
        cells_y = pl.pallas_call(
            functools.partial(y_back_kernel, kyl),
            out_shape=jax.ShapeDtypeStruct((cols, 2, kzl * channels, cells), F32),
            in_specs=[vmem] * 3,
            out_specs=vmem,
            scratch_shapes=[pltpu.VMEM((kzl * channels, 3 * kyl * rows * 2 * a), BF16)],
            compiler_params=big,
        )(by_cells, jnp.asarray(ybh), jnp.asarray(ybl))
        pencils_z = lax.all_to_all(cells_y, "col", 0, 0, tiled=True).reshape(cols * 2 * kzl * channels, cells)
        block = 4
        whole = lambda *shape: pl.BlockSpec(shape, lambda i: (0,) * len(shape))
        features = pl.pallas_call(
            functools.partial(z_back_kernel, channels, block),
            grid=(channels // block,),
            out_shape=jax.ShapeDtypeStruct((channels, cells, nz), BF16),
            in_specs=[
                whole(*pencils_z.shape), whole(width_in, cells, nz), whole(width_in, cells, nz),
                smem, smem, smem, whole(*zb3.shape),
            ],
            out_specs=pl.BlockSpec((block, cells, nz), lambda i: (i, 0, 0)),
            scratch_shapes=[pltpu.VMEM((width_in, cells, nz), F32)],
            compiler_params=big,
        )(
            pencils_z, vel.reshape(width_in, cells, nz), tend.reshape(width_in, cells, nz),
            step.reshape(1), combined, offset, jnp.asarray(zb3),
        )
        results.append(features.reshape(channels, a, b, nz))
    return jnp.stack(results, 0)


def solution(mesh):
    in_specs = (
        P(None, None, "row", "col", None),
        P(None, None, "row", "col", None),
        P(),
        P(),
        P(),
        P(None, "row", "col", None, None),
        P(),
        P(),
    )
    out_specs = P(None, None, "row", "col", None)
    return jax.shard_map(
        per_device, mesh=mesh, in_specs=in_specs, out_specs=out_specs, check_vma=False
    )
```

profile of v0, /device:TPU:0, one launch (start us, length us, event | category | flops | bytes accessed | tf_op | source)
XLA Modules:
  0.0 78.3 jit_solution(3222694749405339193)
XLA Ops:
  0.0 0.0 copy-start
  0.7 1.2 %multiply_add_fusion = f32[1,3,8,16,256]{4,3,2,1,0:T(8,128)S(1)} fusion(f32[1,3,8,16,256]{4,3,2,1,0:T(8,128)} %param.18, f32[1,3,8,16,256]{4,3,2,1,0:T(8,128)} %param.19, f32[]{:T(128)} %bitcast.68), kind=kLoop, calls=%fused_computation.11 | loop fusion | flops 196608 | bytes 1179652 | tf_op jit(solution)/shard_map/add | solution.py:212
  1.9 2.0 %fusion.12 = f32[64,384]{1,0:T(8,128)} fusion(f32[64,256]{1,0:T(8,128)} %constant.36.clone, f32[384,256]{1,0:T(8,128)S(1)} %bitcast.75), kind=kOutput, calls=%fused_computation.26 | convolution fusion | flops 75497472 | bytes 557056 | tf_op jit(solution)/shard_map/dot_general | solution.py:213
  3.9 5.2 %all-to-all-start = ((f32[4,16,384]{2,1,0:T(8,128)}), f32[4,16,384]{2,1,0:T(8,128)S(1)}, u32[]{:S(2)}, u32[]{:S(2)}) async-start(f32[4,16,384]{2,1,0:T(8,128)} %bitcast.2), calls=%async_computation | async-start | bytes 196608 | tf_op jit(solution)/shard_map/all_to_all | solution.py:214
  9.1 0.2 broadcast_in_dim.19
  9.3 0.2 tile.23
  9.6 0.2 copy.36
  9.8 0.0 copy-start.11
  9.8 0.0 copy-done.14
  9.8 0.0 copy-done.12
  9.8 0.1 copy.35
  9.9 0.1 broadcast_in_dim.18
  10.0 0.1 tile.20
  10.1 0.1 reduce-precision_convert_fusion
  10.2 0.0 copy-start.17
  10.2 4.8 %convolution_bitcast_fusion = f32[2048,256]{0,1:T(8,128)} fusion(bf16[2048,1024]{1,0:T(8,128)(2,1)} %bitcast.77, bf16[1024,128]{1,0:T(8,128)(2,1)S(1)} %get-tuple-element.6, bf16[1024,128]{1,0:T(8,128)(2,1)S(1)} %get-tuple-element.5), kind=kOutput, calls=%fused_computation | convolution fusion | flops 1074790400 | bytes 6815744 | tf_op jit(solution)/shard_map/dot_general | solution.py:43
  15.1 0.0 all-to-all-done
  15.1 0.0 copy-done.11
  15.1 1.1 %convolution_bitcast_fusion.1 = f32[2,256,2,3,8]{1,4,0,3,2:T(8,128)S(1)} fusion(f32[2,256,4,128,1,1]{3,1,2,0,5,4:T(8,128)S(1)} %copy-done.11, f32[4,16,384]{2,1,0:T(8,128)S(1)} %all-to-all-done), kind=kOutput, calls=%fused_computation.1 | convolution fusion | flops 150994944 | bytes 1245184 | tf_op jit(solution)/shard_map/pgsn,srkjn->pgrjk/dot_general | solution.py:216
  16.2 0.1 reshape.70
  16.3 0.1 copy.34
  16.4 0.8 reshape.80
  17.2 4.9 %all-to-all-start.1 = ((f32[8,1,1536]{2,1,0:T(1,128)}), f32[8,1,1536]{2,1,0:T(1,128)S(1)}, u32[]{:S(2)}, u32[]{:S(2)}) async-start(f32[8,1,1536]{2,1,0:T(1,128)} %reshape.80), calls=%async_computation.1 | async-start | bytes 98304 | tf_op jit(solution)/shard_map/all_to_all | solution.py:220
  22.1 0.6 and_select_fusion.flag_ref
  22.7 2.0 %copy.37 = f32[2048,256]{1,0:T(8,128)S(1)} copy(f32[2048,256]{0,1:T(8,128)} %convolution_bitcast_fusion) | data formatting | bytes 4194304 | tf_op jit(solution)/shard_map/dot_general | solution.py:43
  24.6 3.3 %all-to-all-done.1 = f32[8,1,1536]{2,1,0:T(1,128)S(1)} async-done(((f32[8,1,1536]{2,1,0:T(1,128)}), f32[8,1,1536]{2,1,0:T(1,128)S(1)}, u32[]{:S(2)}, u32[]{:S(2)}) %all-to-all-start.1) | async-done | bytes 49184 | tf_op jit(solution)/shard_map/all_to_all | solution.py:220
  27.9 0.5 broadcast.6
  28.4 1.3 %reduce = f32[8,1536]{1,0:T(8,128)} reduce(f32[8,1,1536]{2,1,0:T(1,128)S(1)} %all-to-all-done.1, f32[]{:T(128)} %broadcast.6), dimensions={1}, to_apply=%all_to_all.13.reduce_sub_computation | reduce | bytes 98308 | tf_op jit(solution)/shard_map/all_to_all | solution.py:220
  29.7 1.0 %reshape.81.u_ref = f32[8,32,48]{2,1,0:T(8,128)S(1)} reshape(f32[8,1536]{1,0:T(8,128)} %reduce) | data formatting | bytes 98304
  30.7 0.0 copy-start.6
  30.7 0.0 copy-start.8
  30.7 0.9 %copy-done.8 = bf16[128,192]{1,0:T(8,128)(2,1)S(1)} copy-done((bf16[128,192]{1,0:T(8,128)(2,1)S(1)}, bf16[128,192]{1,0:T(8,128)(2,1)}, u32[]{:S(2)}) %copy-start.8) | copy-done | bytes 49176
  31.6 0.8 copy-done.9
  32.4 0.7 copy-done.10
  33.0 1.6 %shard_map.172 = f32[8,16,1024]{2,1,0:T(8,128)S(1)} custom-call(f32[8,32,48]{2,1,0:T(8,128)S(1)} %reshape.81.u_ref, f32[2,1024,256]{2,1,0:T(8,128)S(1)} %bitcast.69, f32[64,64]{1,0:T(8,128)S(1)} %copy-done.9, bf16[48,2048]{1,0:T(8,128)(2,1)S(1)} %copy-done.3, bf16[48,2048]{1,0:T(8,128)(2,1)S(1)} %copy-done.4, f32[1,128]{1,0:T(1,128)S(1)} %copy-done.10, ...), custom_call_target="tpu_custom_call" | custom-call | tf_op jit(solution)/shard_map/pallas_call | solution.py:221
  34.6 0.0 copy-start.15
  34.7 0.0 copy-start.16
  34.7 0.0 copy-start.13
  34.7 0.0 copy-start.7
  34.7 17.9 %all_to_all.20 = f32[8,16,1024]{2,1,0:T(8,128)S(1)} all-to-all(f32[8,16,1024]{2,1,0:T(8,128)S(1)} %shard_map.172), channel_id=1, replica_groups=mesh['row'=8,'col'=4] {'row'}, dimensions={0} | all-to-all | bytes 1048576 | tf_op jit(solution)/shard_map/all_to_all | solution.py:229
  52.6 2.0 %shard_map.173 = f32[4,2,256,128]{3,2,1,0:T(8,128)} custom-call(f32[128,1024]{1,0:T(8,128)S(1)} %bitcast.71, bf16[4,16,1024]{2,1,0:T(8,128)(2,1)S(1)} %copy-done.5, bf16[4,16,1024]{2,1,0:T(8,128)(2,1)S(1)} %copy-done.6), custom_call_target="tpu_custom_call" | custom-call | tf_op jit(solution)/shard_map/pallas_call | solution.py:231
  54.6 4.2 %all-to-all-start.3 = ((f32[4,2,256,128]{3,2,1,0:T(8,128)}), f32[4,2,256,128]{3,2,1,0:T(8,128)S(1)}, u32[]{:S(2)}, u32[]{:S(2)}) async-start(f32[4,2,256,128]{3,2,1,0:T(8,128)} %shard_map.173), calls=%async_computation.3 | async-start | bytes 2097152 | tf_op jit(solution)/shard_map/all_to_all | solution.py:239
  58.8 0.0 copy-done.15
  58.8 0.1 fusion.off_ref
  58.9 0.1 fusion.13.comb_ref
  59.1 13.0 %all-to-all-done.3 = f32[4,2,256,128]{3,2,1,0:T(8,128)S(1)} async-done(((f32[4,2,256,128]{3,2,1,0:T(8,128)}), f32[4,2,256,128]{3,2,1,0:T(8,128)S(1)}, u32[]{:S(2)}, u32[]{:S(2)}) %all-to-all-start.3) | async-done | bytes 1048608 | tf_op jit(solution)/shard_map/all_to_all | solution.py:239
  72.1 0.0 copy-done.2
  72.1 6.2 %shard_map.174 = bf16[32,128,256]{2,1,0:T(8,128)(2,1)} custom-call(f32[2048,128]{1,0:T(8,128)S(1)} %bitcast.70, f32[3,128,256]{2,1,0:T(8,128)S(1)} %bitcast.72, f32[3,128,256]{2,1,0:T(8,128)S(1)} %bitcast.73, f32[1]{0:T(128)} %copy.49.step_ref, f32[32,3]{1,0:T(8,128)S(1)} %fusion.13.comb_ref, f32[32]{0:T(128)S(1)} %fusion.off_ref, bf16[192,256]{1,0:T(8,128)(2,1)S(1)} %copy-done.7), custom_call_target="tpu_custom_call" | custom-call | tf_op jit(solution)/shard_map/pallas_call | solution.py:242
  (25 shorter events, 0.1 us)
Async XLA Ops:
  0.0 58.8 %copy-start = (f32[32,32]{1,0:T(8,128)S(1)}, f32[32,32]{1,0:T(8,128)}, u32[]{:S(2)}) copy-start(f32[32,32]{1,0:T(8,128)} %param.24) | copy-start | bytes 12292
  0.0 9.8 %copy-start.14 = (f32[32]{0:T(128)S(1)}, f32[32]{0:T(128)}, u32[]{:S(2)}) copy-start(f32[32]{0:T(128)} %param.22) | copy-start | bytes 388
  0.0 9.8 %copy-start.12 = (f32[32,3]{0,1:T(4,128)S(1)}, f32[32,3]{0,1:T(4,128)}, u32[]{:S(2)}) copy-start(f32[32,3]{0,1:T(4,128)} %param.21) | copy-start | bytes 1156
  3.9 11.2 %all-to-all-start = ((f32[4,16,384]{2,1,0:T(8,128)}), f32[4,16,384]{2,1,0:T(8,128)S(1)}, u32[]{:S(2)}, u32[]{:S(2)}) async-start(f32[4,16,384]{2,1,0:T(8,128)} %bitcast.2), calls=%async_computation | async-start | bytes 196608 | tf_op jit(solution)/shard_map/all_to_all | solution.py:214
  9.8 5.3 %copy-start.11 = (f32[2,256,4,128,1,1]{3,1,2,0,5,4:T(8,128)S(1)}, f32[2,256,4,128,1,1]{3,1,2,0,5,4:T(8,128)}, u32[]{:S(2)}) copy-start(f32[2,256,4,128,1,1]{3,1,2,0,5,4:T(8,128)} %constant.46) | copy-start | bytes 3145732
  10.2 11.9 %copy-start.17 = (pred[1,128]{1,0:T(4,128)(4,1)S(1)}, pred[1,128]{1,0:T(4,128)(4,1)}, u32[]{:S(2)}) copy-start(pred[1,128]{1,0:T(4,128)(4,1)} %constant.35.clone) | copy-start | bytes 388
  15.0 15.7 %copy-start.3 = (bf16[48,2048]{1,0:T(8,128)(2,1)S(1)}, bf16[48,2048]{1,0:T(8,128)(2,1)}, u32[]{:S(2)}) copy-start(bf16[48,2048]{1,0:T(8,128)(2,1)} %constant.39.clone.selc_ref) | copy-start | bytes 589828
  15.0 15.7 %copy-start.4 = (bf16[48,2048]{1,0:T(8,128)(2,1)S(1)}, bf16[48,2048]{1,0:T(8,128)(2,1)}, u32[]{:S(2)}) copy-start(bf16[48,2048]{1,0:T(8,128)(2,1)} %constant.40.clone.sels_ref) | copy-start | bytes 589828
  17.2 10.7 %all-to-all-start.1 = ((f32[8,1,1536]{2,1,0:T(1,128)}), f32[8,1,1536]{2,1,0:T(1,128)S(1)}, u32[]{:S(2)}, u32[]{:S(2)}) async-start(f32[8,1,1536]{2,1,0:T(1,128)} %reshape.80), calls=%async_computation.1 | async-start | bytes 98304 | tf_op jit(solution)/shard_map/all_to_all | solution.py:220
  22.7 29.9 %copy-start.5 = (bf16[4,16,1024]{2,1,0:T(8,128)(2,1)S(1)}, bf16[4,16,1024]{2,1,0:T(8,128)(2,1)}, u32[]{:S(2)}) copy-start(bf16[4,16,1024]{2,1,0:T(8,128)(2,1)} %constant.42.clone.yh_ref) | copy-start | bytes 393220
  29.7 42.3 %copy-start.1 = (f32[1,3,8,16,256]{4,3,2,1,0:T(8,128)S(1)}, f32[1,3,8,16,256]{4,3,2,1,0:T(8,128)}, u32[]{:S(2)}) copy-start(f32[1,3,8,16,256]{4,3,2,1,0:T(8,128)} %param.18) | copy-start | bytes 1179652
  29.7 42.3 %copy-start.2 = (f32[1,3,8,16,256]{4,3,2,1,0:T(8,128)S(1)}, f32[1,3,8,16,256]{4,3,2,1,0:T(8,128)}, u32[]{:S(2)}) copy-start(f32[1,3,8,16,256]{4,3,2,1,0:T(8,128)} %param.19) | copy-start | bytes 1179652
  30.7 21.9 %copy-start.6 = (bf16[4,16,1024]{2,1,0:T(8,128)(2,1)S(1)}, bf16[4,16,1024]{2,1,0:T(8,128)(2,1)}, u32[]{:S(2)}) copy-start(bf16[4,16,1024]{2,1,0:T(8,128)(2,1)} %constant.43.clone.yl_ref) | copy-start | bytes 393220
  30.7 0.9 %copy-start.8 = (bf16[128,192]{1,0:T(8,128)(2,1)S(1)}, bf16[128,192]{1,0:T(8,128)(2,1)}, u32[]{:S(2)}) copy-start(bf16[128,192]{1,0:T(8,128)(2,1)} %constant.41.clone.xb_ref) | copy-start | bytes 147460
  31.6 0.8 copy-start.9
  32.4 0.7 copy-start.10
  34.6 24.1 %copy-start.15 = (f32[32]{0:T(128)S(1)}, f32[32]{0:T(128)}, u32[]{:S(2)}) copy-start(f32[32]{0:T(128)} %param.22) | copy-start | bytes 388
  34.7 24.1 %copy-start.16 = (f32[32]{0:T(128)S(1)}, f32[32]{0:T(128)}, u32[]{:S(2)}) copy-start(f32[32]{0:T(128)} %param.25) | copy-start | bytes 388
  34.7 24.3 %copy-start.13 = (f32[32,3]{0,1:T(4,128)S(1)}, f32[32,3]{0,1:T(4,128)}, u32[]{:S(2)}) copy-start(f32[32,3]{0,1:T(4,128)} %param.21) | copy-start | bytes 1156
  34.7 37.4 %copy-start.7 = (bf16[192,256]{1,0:T(8,128)(2,1)S(1)}, bf16[192,256]{1,0:T(8,128)(2,1)}, u32[]{:S(2)}) copy-start(bf16[192,256]{1,0:T(8,128)(2,1)} %constant.44.clone.tz_ref) | copy-start | bytes 294916
  54.6 17.4 %all-to-all-start.3 = ((f32[4,2,256,128]{3,2,1,0:T(8,128)}), f32[4,2,256,128]{3,2,1,0:T(8,128)S(1)}, u32[]{:S(2)}, u32[]{:S(2)}) async-start(f32[4,2,256,128]{3,2,1,0:T(8,128)} %shard_map.173), calls=%async_computation.3 | async-start | bytes 2097152 | tf_op jit(solution)/shard_map/all_to_all | solution.py:239
where the time goes:
time: 79 us; the launch traced here: 78.3 us
  blocking collectives  17.9 us (23%)
  waiting for transfers between devices  16.2 us (21%)
  starting transfers between devices  14.2 us (18%)
  Pallas kernels  9.85 us (12%)
  matrix products  8.19 us (10%)
  local copies, waits for them, and re-layouts  7.73 us (10%)
  other arithmetic  3.21 us (4%)
  between operations  0.94 us (1%)
    all_to_all x1, blocking collectives, per_device(): by_cells = lax.all_to_all(cells_x, 'row', 0, 0, tiled=True)  17.9 us
    all_to_all x1, waiting for transfers between devices, per_device(): lax.all_to_all(cells_y, 'col', 0, 0, tiled=True)  13 us
    pallas_call x1, Pallas kernels, per_device(): pl.pallas_call(functools.partial(z_back_kernel, channels, block), grid=(c...  6.21 us
    all_to_all x1, starting transfers between devices, per_device(): lax.all_to_all(z_modes.reshape(cols, 2 * kzl, width_in * cells), 'col', 0...  5.19 us
    all_to_all x1, starting transfers between devices, per_device(): pencils_x = lax.all_to_all(by_y, 'row', 0, 0, tiled=True)  4.88 us
    dot_general x1, matrix products, dot(): return jnp.dot(a, b, preferred_element_type=F32)  4.84 us
    all_to_all x1, starting transfers between devices, per_device(): lax.all_to_all(cells_y, 'col', 0, 0, tiled=True)  4.18 us
    unnamed x38, local copies, waits for them, and re-layouts  4.12 us
  transfers between devices with their start and end apart: 3, of which 2 were waited for; matrix products, arithmetic and copies ran while one was open for 11% of the time, Pallas kernels for 0%

commit v1 on v0

v1 whole, which is shorter than its diff:
```python
import functools
import math

import jax
import jax.numpy as jnp
import numpy as np
from jax import lax
from jax.experimental import pallas as pl
from jax.experimental.pallas import tpu as pltpu
from jax.sharding import PartitionSpec as P

KX = 32
KY = 32
KZ = 32
HIGHEST = lax.Precision.HIGHEST
F32 = jnp.float32
BF16 = jnp.bfloat16


def waves(count):
    index = np.arange(count)
    return np.where(index < count // 2, index, index - count)


def trig(wave, length):
    angle = ((wave[:, None] * np.arange(length)[None, :]) % length) * (2.0 * math.pi / length)
    return np.cos(angle), np.sin(angle)


def np_halves(table):
    table = np.asarray(table, np.float32)
    high = table.astype(jnp.bfloat16)
    low = (table - high.astype(np.float32)).astype(jnp.bfloat16)
    return high, low


def split(x):
    high = x.astype(BF16)
    return high, (x - high.astype(F32)).astype(BF16)


def dot(a, b):
    return jnp.dot(a, b, preferred_element_type=F32)


MESH = pl.DeviceIdType.MESH


def layer_kernel(
    kyl, kzl, part, scale, vel_ref, tend_ref, step_ref, zf_ref, yfh_ref, yfl_ref, w_ref, lift_ref, xf_ref, selc_ref,
    sels_ref, flag_ref, xb_ref, yh_ref, yl_ref, out_ref, w_vmem, wl_ref, zsend, zrecv, ypad, ysend, yrecv, m_ref, xsend, xrecv,
    lhs_ref, csend, w_sem, z_ss, z_rs, y_ss, y_rs, x_ss, x_rs, c_ss, c_rs,
):
    rows, cols = lax.axis_size("row"), lax.axis_size("col")
    my_row, my_col = lax.axis_index("row"), lax.axis_index("col")
    width_in, cells, _ = vel_ref.shape
    rk = zf_ref.shape[0] // cols
    a = ysend.shape[1] // kyl
    b = cells // a
    modes = kyl * kzl * KX
    chunks = xsend.shape[0]

    load = pltpu.make_async_copy(w_ref, w_vmem, w_sem)
    load.start()
    barrier = pltpu.get_barrier_semaphore()
    row_peers = [lax.rem(my_row + i, rows) for i in range(1, rows)]
    col_peers = [lax.rem(my_col + i, cols) for i in range(1, cols)]
    for peer in row_peers:
        pl.semaphore_signal(barrier, inc=1, device_id={"row": peer}, device_id_type=MESH)
    for peer in col_peers:
        pl.semaphore_signal(barrier, inc=1, device_id={"col": peer}, device_id_type=MESH)

    for j in range(width_in):
        adv = vel_ref[j] + step_ref[0] * tend_ref[j]
        z = lax.dot_general(
            zf_ref[...], adv, (((1,), (1,)), ((), ())), precision=HIGHEST, preferred_element_type=F32
        )
        zsend[:, j * rk:(j + 1) * rk, :] = z.reshape(cols, rk, cells)
    pl.semaphore_wait(barrier, rows + cols - 2)
    z_copies = []
    for i, peer in enumerate(col_peers):
        copy = pltpu.make_async_remote_copy(
            zsend.at[peer], zrecv.at[my_col], z_ss.at[i], z_rs.at[i], device_id={"col": peer}, device_id_type=MESH
        )
        copy.start()
        z_copies.append(copy)
    zrecv[pl.ds(my_col, 1)] = zsend[pl.ds(my_col, 1)]

    load.wait()
    step_rows = modes // 2
    half_lanes = lift_ref.shape[1] // 2

    def weigh(n):
        at = slice(n * step_rows, (n + 1) * step_rows)
        both = dot(w_vmem[at, :], lift_ref[...])
        wl_ref[at, :] = both[:, :half_lanes] + both[:, half_lanes:]

    weigh(0)
    weigh(1)
    for copy in z_copies:
        copy.wait_recv()

    x = jnp.concatenate([zrecv[s] for s in range(cols)], 1)
    xh, xl = split(x)
    y = dot(xh, yfh_ref[...]) + dot(xl, yfh_ref[...]) + dot(xh, yfl_ref[...])
    lanes = rows * kyl * a
    ypad[...] = jnp.zeros_like(ypad)
    low_rows = lax.broadcasted_iota(jnp.int32, (rk, lanes), 0) < rk // 2
    for j in range(width_in):
        block = y[j * rk:(j + 1) * rk]
        turned = pltpu.roll(block[:, lanes:], rk // 2, 0)
        ypad[j * rk:(j + 1) * rk, :] = block[:, :lanes] + jnp.where(low_rows, turned, -turned)
    ysend[...] = jnp.transpose(ypad[...]).reshape(ysend.shape)
    y_copies = []
    for i, peer in enumerate(row_peers):
        copy = pltpu.make_async_remote_copy(
            ysend.at[peer], yrecv.at[my_row], y_ss.at[i], y_rs.at[i], device_id={"row": peer}, device_id_type=MESH
        )
        copy.start()
        y_copies.append(copy)
    yrecv[pl.ds(my_row, 1)] = ysend[pl.ds(my_row, 1)]
    weigh(2)
    weigh(3)
    for copy in y_copies:
        copy.wait_recv()

    cos_parts, sin_parts = [], []
    for l in range(kyl):
        u = yrecv[:, l * a:(l + 1) * a, :].reshape(rows * a, yrecv.shape[2])
        q = jnp.dot(xf_ref[...], u, precision=HIGHEST, preferred_element_type=F32) * scale
        cos_parts.append(q[:KX])
        sin_parts.append(q[KX:])
    ch, cl = split(jnp.concatenate(cos_parts, 0))
    sh, sl = split(jnp.concatenate(sin_parts, 0))
    selc, sels = selc_ref[...], sels_ref[...]
    amp = dot(ch, selc) + dot(cl, selc) + dot(sh, sels) + dot(sl, sels)
    lane = lax.broadcasted_iota(jnp.int32, (KX, 128), 1)
    row = lax.broadcasted_iota(jnp.int32, (KX, 128), 0)
    quarter = lane // 32
    order = [(l, c * part + k) for c in range(chunks) for l in range(kyl) for k in range(part)]
    chunk_lanes = xsend.shape[3]
    x_copies = []
    for c in range(chunks):
        for group in range(chunk_lanes // 128):
            packed_r = packed_i = None
            for q in range(4):
                l, k = order[(c * chunk_lanes // 128 + group) * 4 + q]
                ar = amp[l * KX:(l + 1) * KX, k * 256:k * 256 + 128]
                ai = amp[l * KX:(l + 1) * KX, k * 256 + 128:k * 256 + 256]
                if l == 0 and k == 0:
                    ar = ar + jnp.where(row == 0, flag_ref[...], 0.0)
                at = (l * kzl + k) * KX
                wr = wl_ref[at:at + KX, :]
                wi = wl_ref[modes + at:modes + at + KX, :]
                pr = wr * ar - wi * ai
                pi = wr * ai + wi * ar
                pr = pr + pltpu.roll(pr, 64, 1)
                pi = pi + pltpu.roll(pi, 64, 1)
                pr = pr + pltpu.roll(pr, 32, 1)
                pi = pi + pltpu.roll(pi, 32, 1)
                packed_r = pr if q == 0 else jnp.where(quarter == q, pr, packed_r)
                packed_i = pi if q == 0 else jnp.where(quarter == q, pi, packed_i)
            at = slice(group * 128, (group + 1) * 128)
            mh, ml = split(jnp.concatenate([packed_r, packed_i], 0))
            m_ref[0:2 * KX, at] = mh
            m_ref[2 * KX:4 * KX, at] = ml
            m_ref[4 * KX:6 * KX, at] = mh
        xsend[c] = dot(xb_ref[...], m_ref[...]).reshape(xsend.shape[1:])
        started = []
        for i, peer in enumerate(row_peers):
            copy = pltpu.make_async_remote_copy(
                xsend.at[c, peer], xrecv.at[c, my_row], x_ss.at[c, i], x_rs.at[c, i],
                device_id={"row": peer}, device_id_type=MESH,
            )
            copy.start()
            started.append(copy)
        xrecv[c, pl.ds(my_row, 1)] = xsend[c, pl.ds(my_row, 1)]
        x_copies.append(started)

    total = rows * 2 * a
    ko = chunk_lanes // kyl
    pairs = 2 * rows
    width = 2 * cells
    xr = lax.broadcasted_iota(jnp.int32, (pairs, a, width), 1)
    xl = (lax.broadcasted_iota(jnp.int32, (pairs, a, width), 2) // b) % a
    same = xr == xl

    def expand(table):
        full = jnp.where(same, table.astype(F32)[:, None, :], 0.0)
        return full.reshape(total, width).astype(BF16)

    c_copies = []
    for c in range(chunks):
        for copy in x_copies[c]:
            copy.wait_recv()
        for l in range(kyl):
            held = xrecv[c, :, :, l * ko:(l + 1) * ko].reshape(total, ko)
            th, tl = split(jnp.transpose(held))
            lhs_ref[:, l * total:(l + 1) * total] = th
            lhs_ref[:, (kyl + l) * total:(kyl + l + 1) * total] = tl
            lhs_ref[:, (2 * kyl + l) * total:(2 * kyl + l + 1) * total] = th
        at = pl.ds(c * ko, ko)
        for i in list(range(1, cols)) + [0]:
            d = lax.rem(my_col + i, cols)
            high = [expand(yh_ref[d, l]) for l in range(kyl)]
            low = [expand(yl_ref[d, l]) for l in range(kyl)]
            acc = dot(lhs_ref[...], jnp.concatenate(high + high + low, 0))
            if i == 0:
                for v in range(2):
                    out_ref[pl.ds(my_col, 1), v, at, :] = acc[:, v * cells:(v + 1) * cells][None]
            else:
                for v in range(2):
                    csend[c, i - 1, v] = acc[:, v * cells:(v + 1) * cells]
                copy = pltpu.make_async_remote_copy(
                    csend.at[c, i - 1], out_ref.at[my_col, :, at, :], c_ss.at[c, i - 1], c_rs.at[c, i - 1],
                    device_id={"col": d}, device_id_type=MESH,
                )
                copy.start()
                c_copies.append(copy)
    for copy in c_copies:
        copy.wait_recv()
    for copy in z_copies + y_copies + [copy for started in x_copies for copy in started] + c_copies:
        copy.wait_send()


def z_back_kernel(channels, block, d_ref, vel_ref, tend_ref, step_ref, comb_ref, off_ref, tz_ref, out_ref, adv_ref):
    first = pl.program_id(0)
    depth = d_ref.shape[0] // channels

    @pl.when(first == 0)
    def _():
        adv_ref[...] = vel_ref[...] + step_ref[0] * tend_ref[...]

    for i in range(block):
        o = first * block + i
        high, low = split(d_ref[pl.ds(o, depth, stride=channels), :])
        lhs = jnp.concatenate([high, low, high], 0)
        spectral = lax.dot_general(lhs, tz_ref[...], (((0,), (0,)), ((), ())), preferred_element_type=F32)
        x = spectral + off_ref[o]
        for j in range(adv_ref.shape[0]):
            x = x + comb_ref[o, j] * adv_ref[j]
        inner = x * (0.7978845608028654 + 0.035677408136300125 * (x * x))
        half = 0.5 * x
        out_ref[i] = (half + half * jnp.tanh(inner)).astype(BF16)


def per_device(
    velocity, tendency, step_size, lift_weight, lift_bias, spectral_weight, local_weight, local_bias
):
    samples, width_in, a, b, nz = velocity.shape
    channels = lift_weight.shape[0]
    rows, cols = lax.axis_size("row"), lax.axis_size("col")
    full_x, full_y = a * rows, b * cols
    kzl, kyl = KZ // cols, KY // rows
    modes = kyl * kzl * KX
    cells = a * b
    vmem = pl.BlockSpec(memory_space=pltpu.VMEM)
    smem = pl.BlockSpec(memory_space=pltpu.SMEM)
    big = pltpu.CompilerParams(vmem_limit_bytes=48 * 1024 * 1024)

    lift4 = jnp.concatenate([lift_weight, lift_bias[:, None]], 1)
    group = width_in + 1
    eye = jnp.eye(channels, dtype=F32)
    lift_lanes = jnp.repeat(lift4, channels, axis=1)
    lift_full = jnp.tile(lift_lanes, (channels, 1))
    own = jnp.tile(jnp.repeat(eye, channels, axis=0), (1, group))
    masked = lift_full * own
    high = lax.reduce_precision(masked, 8, 7)
    lh, ll = high.astype(BF16), (masked - high).astype(BF16)
    lift_map = jnp.concatenate([lh, ll], 1)
    stored = spectral_weight.reshape(2 * modes, channels * channels)

    zc, zs = trig(np.arange(KZ), nz)
    rk = 2 * max(kzl, 4)
    zf = np.zeros((cols, 2, rk // 2, nz), np.float32)
    zf[:, :, :kzl] = np.stack([zc, -zs], 0).reshape(2, cols, kzl, nz).transpose(1, 0, 2, 3)
    zf = zf.reshape(cols * rk, nz)
    yc, ys = trig(waves(KY), full_y)
    xc, xs = trig(waves(KX), full_x)
    xf = np.concatenate([xc, xs], 0).astype(np.float32)
    selc = np.zeros((128, kzl, 2, group, channels), np.float32)
    sels = np.zeros_like(selc)
    for j in range(width_in):
        for k in range(kzl):
            re, im = j * rk + k, j * rk + rk // 2 + k
            selc[re, k, 0, j] = 1
            selc[im, k, 1, j] = 1
            sels[im, k, 0, j] = 1
            sels[re, k, 1, j] = -1
    selc = selc.reshape(128, -1)
    sels = sels.reshape(128, -1)
    xb = np.stack([np.stack([xc, -xs], 0), np.stack([xs, xc], 0)], 0)
    xb = xb.reshape(2, 2, KX, rows, a).transpose(3, 0, 4, 1, 2).reshape(rows * 2 * a, 2 * KX)
    xbh, xbl = np_halves(xb)
    xb3 = np.concatenate([xbh, xbh, xbl], 1)
    yb = np.stack([np.stack([yc, ys], 0), np.stack([-ys, yc], 0)], 0)
    yb = yb.reshape(2, 2, rows, kyl, cols, b).transpose(4, 3, 2, 0, 1, 5)
    yb = np.broadcast_to(yb[..., None, :], (cols, kyl, rows, 2, 2, a, b)).reshape(cols, kyl, rows * 2, 2 * cells)
    ybh, ybl = np_halves(yb)
    twice = np.where(np.arange(KZ) == 0, 1.0, 2.0)[:, None]
    zb = np.stack([twice * zc, -twice * zs], 0).reshape(2, cols, kzl, nz).transpose(1, 0, 2, 3).reshape(2 * KZ, nz)
    zbh, zbl = np_halves(zb)
    zb3 = np.concatenate([zbh, zbh, zbl], 0)
    yf = np.stack([yc, ys], 0).reshape(2, rows, kyl, 1, cols, 1, b)
    yf = (yf * np.eye(a).reshape(1, 1, 1, a, 1, a, 1)).reshape(2 * rows * kyl * a, cols * cells).T
    yfh, yfl = np_halves(yf)

    combined = jnp.dot(local_weight, lift_weight, precision=HIGHEST)
    offset = jnp.dot(local_weight, lift_bias, precision=HIGHEST) + local_bias
    origin = (lax.axis_index("row") == 0) & (lax.axis_index("col") == 0)
    last = np.arange(group * channels)[None, :] >= width_in * channels
    flag = jnp.where(jnp.asarray(last) & origin, 1.0, 0.0).astype(F32)

    results = []
    for sample in range(samples):
        vel = velocity[sample].reshape(width_in, cells, nz)
        tend = tendency[sample].reshape(width_in, cells, nz)
        step = step_size[sample].reshape(1)
        part = min(kzl, 4)
        chunks = kzl // part
        chunk_lanes = kyl * part * channels
        dma = lambda *shape: pltpu.SemaphoreType.DMA(shape)
        pencils_z = pl.pallas_call(
            functools.partial(layer_kernel, kyl, kzl, part, 1.0 / (full_x * full_y * nz)),
            out_shape=jax.ShapeDtypeStruct((cols, 2, kzl * channels, cells), F32),
            in_specs=[vmem, vmem, smem, vmem, vmem, vmem, pl.BlockSpec(memory_space=pl.ANY)] + [vmem] * 8,
            out_specs=vmem,
            scratch_shapes=[
                pltpu.VMEM(stored.shape, BF16),
                pltpu.VMEM((2 * modes, group * channels), F32),
                pltpu.VMEM((cols, width_in * rk, cells), F32),
                pltpu.VMEM((cols, width_in * rk, cells), F32),
                pltpu.VMEM((128, rows * kyl * a), F32),
                pltpu.VMEM((rows, kyl * a, 128), F32),
                pltpu.VMEM((rows, kyl * a, 128), F32),
                pltpu.VMEM((6 * KX, chunk_lanes), BF16),
                pltpu.VMEM((chunks, rows, 2 * a, chunk_lanes), F32),
                pltpu.VMEM((chunks, rows, 2 * a, chunk_lanes), F32),
                pltpu.VMEM((part * channels, 3 * kyl * rows * 2 * a), BF16),
                pltpu.VMEM((chunks, cols - 1, 2, part * channels, cells), F32),
                pltpu.SemaphoreType.DMA,
                dma(cols - 1), dma(cols - 1), dma(rows - 1), dma(rows - 1),
                dma(chunks, rows - 1), dma(chunks, rows - 1), dma(chunks, cols - 1), dma(chunks, cols - 1),
            ],
            compiler_params=pltpu.CompilerParams(
                vmem_limit_bytes=48 * 1024 * 1024, collective_id=0, has_side_effects=True
            ),
        )(
            vel, tend, step, jnp.asarray(zf), jnp.asarray(yfh), jnp.asarray(yfl), stored, lift_map, jnp.asarray(xf),
            jnp.asarray(selc, BF16), jnp.asarray(sels, BF16), flag, jnp.asarray(xb3), jnp.asarray(ybh), jnp.asarray(ybl),
        )
        pencils_z = pencils_z.reshape(cols * 2 * kzl * channels, cells)
        block = 4
        whole = lambda *shape: pl.BlockSpec(shape, lambda i: (0,) * len(shape))
        features = pl.pallas_call(
            functools.partial(z_back_kernel, channels, block),
            grid=(channels // block,),
            out_shape=jax.ShapeDtypeStruct((channels, cells, nz), BF16),
            in_specs=[
                whole(*pencils_z.shape), whole(width_in, cells, nz), whole(width_in, cells, nz),
                smem, smem, smem, whole(*zb3.shape),
            ],
            out_specs=pl.BlockSpec((block, cells, nz), lambda i: (i, 0, 0)),
            scratch_shapes=[pltpu.VMEM((width_in, cells, nz), F32)],
            compiler_params=big,
        )(
            pencils_z, vel, tend, step, combined, offset, jnp.asarray(zb3),
        )
        results.append(features.reshape(channels, a, b, nz))
    return jnp.stack(results, 0)


def solution(mesh):
    in_specs = (
        P(None, None, "row", "col", None),
        P(None, None, "row", "col", None),
        P(),
        P(),
        P(),
        P(None, "row", "col", None, None),
        P(),
        P(),
    )
    out_specs = P(None, None, "row", "col", None)
    return jax.shard_map(
        per_device, mesh=mesh, in_specs=in_specs, out_specs=out_specs, check_vma=False
    )
```

time: 79 us -> 54.7 us (0.69)
  the two profiles are of different devices: /device:TPU:0 before, /device:TPU:9 now
where the time goes in v1:
time: 54.7 us; the launch traced here: 54.4 us
  Pallas kernels  43.5 us (80%)
  local copies, waits for them, and re-layouts  5.5 us (10%)
  other arithmetic  2.74 us (5%)
  matrix products  1.61 us (3%)
  between operations  1.04 us (2%)
    pallas_call x1, Pallas kernels, per_device(): pl.pallas_call(functools.partial(layer_kernel, kyl, kzl, part, 1.0 / (ful...  37.3 us
    pallas_call x1, Pallas kernels, per_device(): pl.pallas_call(functools.partial(z_back_kernel, channels, block), grid=(c...  6.21 us
    another operation x3, local copies, waits for them, and re-layouts, per_device(): own = jnp.tile(jnp.repeat(eye, channels, axis=0), (1, group))  4.16 us
    convert_element_type x1, other arithmetic, per_device(): lh, ll = (high.astype(BF16), (masked - high).astype(BF16))  1.14 us

profile of v1, /device:TPU:9, one launch (start us, length us, event | category | flops | bytes accessed | tf_op | source)
XLA Modules:
  0.0 54.4 jit_solution(12546370816345428463)
XLA Ops:
  0.0 0.0 copy-start
  0.0 0.0 copy-start.7
  0.0 0.0 copy-start.8
  0.0 0.0 copy-start.10
  0.0 0.0 copy-start.3
  0.0 0.0 copy-start.4
  0.1 0.0 copy-start.12
  0.1 0.0 copy-start.5
  0.1 0.0 copy-start.6
  0.1 0.0 copy-start.11
  0.1 0.0 copy-start.2
  0.1 0.0 copy-start.1
  0.9 0.8 %and_select_fusion.flag_ref = f32[1,128]{1,0:T(1,128)S(1)} fusion(pred[1,128]{1,0:T(4,128)(4,1)} %constant.37.clone, pred[]{:T(512)S(6)} %and.11), kind=kLoop, calls=%fused_computation.10 | loop fusion | flops 256 | bytes 641 | tf_op jit(solution)/shard_map/jit(_where)/select_n | solution.py:312
  1.7 0.0 copy-done
  1.7 0.8 %fusion.off_ref = f32[32]{0:T(128)S(1)} fusion(f32[32]{0:T(128)} %param.26, f32[32,32]{1,0:T(8,128)S(1)} %copy-done, f32[32]{0:T(128)} %param.23), kind=kOutput, calls=%fused_computation.1 | convolution fusion | flops 12320 | bytes 4480 | tf_op jit(solution)/shard_map/dot_general | solution.py:309
  2.5 0.7 %pad_maximum_fusion.1 = f32[32,4]{0,1:T(4,128)S(1)} fusion(f32[32,1]{0,1:T(1,128)} %bitcast.32, f32[32,3]{0,1:T(4,128)} %param.22), kind=kLoop, calls=%fused_computation.9 | loop fusion | flops 128 | bytes 1024 | tf_op jit(solution)/shard_map/concatenate | solution.py:261
  3.3 0.1 copy.22
  3.4 0.8 %fusion.4.comb_ref = f32[32,3]{1,0:T(8,128)S(1)} fusion(f32[32,32]{1,0:T(8,128)S(1)} %copy-done, f32[32,3]{0,1:T(4,128)} %param.22), kind=kOutput, calls=%fused_computation.12 | convolution fusion | flops 36864 | bytes 4864 | tf_op jit(solution)/shard_map/dot_general | solution.py:308
  4.2 0.1 broadcast_in_dim.18
  4.3 0.1 tile.20
  4.4 1.0 %broadcast_in_dim.19 = f32[32,32,32]{1,0,2:T(8,128)} broadcast(f32[32,32]{0,1:T(8,128)S(1)} %fusion.2), dimensions={0,2} | broadcast | bytes 135168 | tf_op jit(solution)/shard_map/broadcast_in_dim | solution.py:266
  5.4 1.3 %tile.23 = f32[1024,32]{0,1:T(8,128)S(1)} reshape(f32[32,32,32]{1,0,2:T(8,128)} %broadcast_in_dim.19) | data formatting | bytes 262144 | tf_op jit(solution)/shard_map/tile | solution.py:266
  6.7 0.8 %tile.24 = f32[1024,4,32]{0,2,1:T(8,128)} broadcast(f32[1024,32]{0,1:T(8,128)S(1)} %tile.23), dimensions={0,2} | broadcast | bytes 655360 | tf_op jit(solution)/shard_map/tile | solution.py:266
  7.5 2.0 %copy.23 = f32[1024,128]{1,0:T(8,128)} copy(f32[1024,128]{0,1:T(8,128)} %bitcast.31) | data formatting | bytes 1048576 | tf_op jit(solution)/shard_map/tile | solution.py:266
  9.5 1.1 %reduce-precision_convert_fusion = (bf16[1024,128]{1,0:T(8,128)(2,1)S(1)}, bf16[1024,128]{1,0:T(8,128)(2,1)S(1)}) fusion(f32[1024,128]{1,0:T(8,128)} %copy.23, f32[32,128]{1,0:T(8,128)S(1)} %tile.20), kind=kLoop, calls=%fused_computation.3 | loop fusion | flops 655360 | bytes 1064960 | tf_op jit(solution)/shard_map/convert_element_type | solution.py:269
  10.7 0.1 pad_maximum_fusion.lift_ref
  10.8 0.0 copy-done.7
  10.8 0.0 copy-done.8
  10.8 0.0 copy-done.10
  10.8 0.0 copy-done.3
  10.8 0.0 copy-done.4
  10.8 0.0 copy-done.12
  10.8 0.0 copy-done.5
  10.8 0.0 copy-done.6
  10.8 0.0 copy-done.11
  10.8 0.0 copy-done.2
  10.9 0.0 copy-done.1
  10.9 0.0 copy-start.9
  10.9 37.3 %shard_map.181 = f32[4,2,256,128]{3,2,1,0:T(8,128)S(1)} custom-call(f32[3,128,256]{2,1,0:T(8,128)S(1)} %bitcast.26, f32[3,128,256]{2,1,0:T(8,128)S(1)} %bitcast.28, f32[1]{0:T(128)S(6)} %copy.26.step_ref, f32[64,256]{1,0:T(8,128)S(1)} %copy-done.11, bf16[512,512]{1,0:T(8,128)(2,1)S(1)} %copy-done.6, bf16[512,512]{1,0:T(8,128)(2,1)S(1)} %copy-done.5, ...), custom_call_target="tpu_custom_call" | custom-call | tf_op jit(solution)/shard_map/pallas_call | solution.py:323
  48.2 0.0 copy-done.9
  48.2 6.2 %shard_map.182 = bf16[32,128,256]{2,1,0:T(8,128)(2,1)} custom-call(f32[2048,128]{1,0:T(8,128)S(1)} %bitcast.25, f32[3,128,256]{2,1,0:T(8,128)S(1)} %bitcast.27, f32[3,128,256]{2,1,0:T(8,128)S(1)} %bitcast.29, f32[1]{0:T(128)S(6)} %copy.26.step_ref, f32[32,3]{1,0:T(8,128)S(1)} %fusion.4.comb_ref, f32[32]{0:T(128)S(1)} %fusion.off_ref, ...), custom_call_target="tpu_custom_call" | custom-call | tf_op jit(solution)/shard_map/pallas_call | solution.py:355
  (1 shorter events, 0.0 us)
Async XLA Ops:
  0.0 1.7 %copy-start = (f32[32,32]{1,0:T(8,128)S(1)}, f32[32,32]{1,0:T(8,128)}, u32[]{:S(2)}) copy-start(f32[32,32]{1,0:T(8,128)} %param.25) | copy-start | bytes 12292
  0.0 10.8 %copy-start.7 = (bf16[4,4,16,256]{3,2,1,0:T(8,128)(2,1)S(1)}, bf16[4,4,16,256]{3,2,1,0:T(8,128)(2,1)}, u32[]{:S(2)}) copy-start(bf16[4,4,16,256]{3,2,1,0:T(8,128)(2,1)} %constant.46.clone.yl_ref) | copy-start | bytes 393220
  0.0 10.8 %copy-start.8 = (bf16[4,4,16,256]{3,2,1,0:T(8,128)(2,1)S(1)}, bf16[4,4,16,256]{3,2,1,0:T(8,128)(2,1)}, u32[]{:S(2)}) copy-start(bf16[4,4,16,256]{3,2,1,0:T(8,128)(2,1)} %constant.45.clone.yh_ref) | copy-start | bytes 393220
  0.0 10.8 %copy-start.10 = (bf16[128,192]{1,0:T(8,128)(2,1)S(1)}, bf16[128,192]{1,0:T(8,128)(2,1)}, u32[]{:S(2)}) copy-start(bf16[128,192]{1,0:T(8,128)(2,1)} %constant.44.clone.xb_ref) | copy-start | bytes 147460
  0.0 10.8 %copy-start.3 = (bf16[128,2048]{1,0:T(8,128)(2,1)S(1)}, bf16[128,2048]{1,0:T(8,128)(2,1)}, u32[]{:S(2)}) copy-start(bf16[128,2048]{1,0:T(8,128)(2,1)} %constant.43.clone.sels_ref) | copy-start | bytes 1572868
  0.0 10.8 %copy-start.4 = (bf16[128,2048]{1,0:T(8,128)(2,1)S(1)}, bf16[128,2048]{1,0:T(8,128)(2,1)}, u32[]{:S(2)}) copy-start(bf16[128,2048]{1,0:T(8,128)(2,1)} %constant.42.clone.selc_ref) | copy-start | bytes 1572868
  0.1 10.8 %copy-start.12 = (f32[64,64]{1,0:T(8,128)S(1)}, f32[64,64]{1,0:T(8,128)}, u32[]{:S(2)}) copy-start(f32[64,64]{1,0:T(8,128)} %constant.41.clone.xf_ref) | copy-start | bytes 49156
  0.1 10.8 %copy-start.5 = (bf16[512,512]{1,0:T(8,128)(2,1)S(1)}, bf16[512,512]{1,0:T(8,128)(2,1)}, u32[]{:S(2)}) copy-start(bf16[512,512]{1,0:T(8,128)(2,1)} %constant.40.clone.yfl_ref) | copy-start | bytes 1572868
  0.1 10.7 %copy-start.6 = (bf16[512,512]{1,0:T(8,128)(2,1)S(1)}, bf16[512,512]{1,0:T(8,128)(2,1)}, u32[]{:S(2)}) copy-start(bf16[512,512]{1,0:T(8,128)(2,1)} %constant.39.clone.yfh_ref) | copy-start | bytes 1572868
  0.1 10.7 %copy-start.11 = (f32[64,256]{1,0:T(8,128)S(1)}, f32[64,256]{1,0:T(8,128)}, u32[]{:S(2)}) copy-start(f32[64,256]{1,0:T(8,128)} %constant.38.clone.zf_ref) | copy-start | bytes 196612
  0.1 10.7 %copy-start.2 = (f32[1,3,8,16,256]{4,3,2,1,0:T(8,128)S(1)}, f32[1,3,8,16,256]{4,3,2,1,0:T(8,128)}, u32[]{:S(2)}) copy-start(f32[1,3,8,16,256]{4,3,2,1,0:T(8,128)} %param.20) | copy-start | bytes 1179652
  0.1 10.7 %copy-start.1 = (f32[1,3,8,16,256]{4,3,2,1,0:T(8,128)S(1)}, f32[1,3,8,16,256]{4,3,2,1,0:T(8,128)}, u32[]{:S(2)}) copy-start(f32[1,3,8,16,256]{4,3,2,1,0:T(8,128)} %param.19) | copy-start | bytes 1179652
  10.9 37.3 %copy-start.9 = (bf16[192,256]{1,0:T(8,128)(2,1)S(1)}, bf16[192,256]{1,0:T(8,128)(2,1)}, u32[]{:S(2)}) copy-start(bf16[192,256]{1,0:T(8,128)(2,1)} %constant.47.clone.tz_ref) | copy-start | bytes 294916

commit v2 on v1

--- a/solution.py
+++ b/solution.py
@@ -46,9 +46,15 @@
 MESH = pl.DeviceIdType.MESH
 
 
+def column(line):
+    n = line.shape[1]
+    own = lax.broadcasted_iota(jnp.int32, (n, n), 0) == lax.broadcasted_iota(jnp.int32, (n, n), 1)
+    return jnp.sum(jnp.where(own, line, 0.0), axis=1, keepdims=True)
+
+
 def layer_kernel(
-    kyl, kzl, part, scale, vel_ref, tend_ref, step_ref, zf_ref, yfh_ref, yfl_ref, w_ref, lift_ref, xf_ref, selc_ref,
-    sels_ref, flag_ref, xb_ref, yh_ref, yl_ref, out_ref, w_vmem, wl_ref, zsend, zrecv, ypad, ysend, yrecv, m_ref, xsend, xrecv,
+    kyl, kzl, part, scale, vel_ref, tend_ref, step_ref, zf_ref, yfh_ref, yfl_ref, w_ref, lw_ref, lb_ref, xf_ref, selc_ref,
+    sels_ref, xb_ref, yh_ref, yl_ref, out_ref, lift_ref, w_vmem, wl_ref, zsend, zrecv, ypad, ysend, yrecv, m_ref, xsend, xrecv,
     lhs_ref, csend, w_sem, z_ss, z_rs, y_ss, y_rs, x_ss, x_rs, c_ss, c_rs,
 ):
     rows, cols = lax.axis_size("row"), lax.axis_size("col")
@@ -85,6 +91,16 @@
         copy.start()
         z_copies.append(copy)
     zrecv[pl.ds(my_col, 1)] = zsend[pl.ds(my_col, 1)]
+
+    channels = lb_ref.shape[1]
+    place = lax.broadcasted_iota(jnp.int32, (channels, 128), 1)
+    base = jnp.broadcast_to(column(lb_ref[...]), (channels, 128))
+    for j in range(width_in):
+        base = jnp.where(place // channels == j, column(lw_ref[j:j + 1, :]), base)
+    for o in range(channels):
+        lh, ll = split(jnp.where(place % channels == o, base, 0.0))
+        lift_ref[o * channels:(o + 1) * channels, :128] = lh
+        lift_ref[o * channels:(o + 1) * channels, 128:] = ll
 
     load.wait()
     step_rows = modes // 2
@@ -137,6 +153,7 @@
     lane = lax.broadcasted_iota(jnp.int32, (KX, 128), 1)
     row = lax.broadcasted_iota(jnp.int32, (KX, 128), 0)
     quarter = lane // 32
+    origin = jnp.where((my_row == 0) & (my_col == 0), 1.0, 0.0).astype(F32)
     order = [(l, c * part + k) for c in range(chunks) for l in range(kyl) for k in range(part)]
     chunk_lanes = xsend.shape[3]
     x_copies = []
@@ -148,7 +165,7 @@
                 ar = amp[l * KX:(l + 1) * KX, k * 256:k * 256 + 128]
                 ai = amp[l * KX:(l + 1) * KX, k * 256 + 128:k * 256 + 256]
                 if l == 0 and k == 0:
-                    ar = ar + jnp.where(row == 0, flag_ref[...], 0.0)
+                    ar = ar + jnp.where((row == 0) & (lane >= width_in * channels), origin, 0.0)
                 at = (l * kzl + k) * KX
                 wr = wl_ref[at:at + KX, :]
                 wi = wl_ref[modes + at:modes + at + KX, :]
@@ -223,22 +240,28 @@
         copy.wait_send()
 
 
-def z_back_kernel(channels, block, d_ref, vel_ref, tend_ref, step_ref, comb_ref, off_ref, tz_ref, out_ref, adv_ref):
+def z_back_kernel(channels, block, d_ref, vel_ref, tend_ref, step_ref, lw_ref, lb_ref, mw_ref, mb_ref, tz_ref, out_ref, adv_ref, line_ref):
     first = pl.program_id(0)
     depth = d_ref.shape[0] // channels
 
     @pl.when(first == 0)
     def _():
         adv_ref[...] = vel_ref[...] + step_ref[0] * tend_ref[...]
+        width_in = lw_ref.shape[0]
+        for j in range(width_in + 1):
+            line = lw_ref[j:j + 1, :] if j < width_in else lb_ref[...]
+            wide = jnp.broadcast_to(column(line), (channels, line_ref.shape[2]))
+            mapped = jnp.dot(mw_ref[...], wide, precision=HIGHEST, preferred_element_type=F32)
+            line_ref[j] = mapped if j < width_in else mapped + column(mb_ref[...])
 
     for i in range(block):
         o = first * block + i
         high, low = split(d_ref[pl.ds(o, depth, stride=channels), :])
         lhs = jnp.concatenate([high, low, high], 0)
         spectral = lax.dot_general(lhs, tz_ref[...], (((0,), (0,)), ((), ())), preferred_element_type=F32)
-        x = spectral + off_ref[o]
+        x = spectral + line_ref[adv_ref.shape[0], pl.ds(o, 1), :]
         for j in range(adv_ref.shape[0]):
-            x = x + comb_ref[o, j] * adv_ref[j]
+            x = x + line_ref[j, pl.ds(o, 1), :] * adv_ref[j]
         inner = x * (0.7978845608028654 + 0.035677408136300125 * (x * x))
         half = 0.5 * x
         out_ref[i] = (half + half * jnp.tanh(inner)).astype(BF16)
@@ -258,16 +281,7 @@
     smem = pl.BlockSpec(memory_space=pltpu.SMEM)
     big = pltpu.CompilerParams(vmem_limit_bytes=48 * 1024 * 1024)
 
-    lift4 = jnp.concatenate([lift_weight, lift_bias[:, None]], 1)
     group = width_in + 1
-    eye = jnp.eye(channels, dtype=F32)
-    lift_lanes = jnp.repeat(lift4, channels, axis=1)
-    lift_full = jnp.tile(lift_lanes, (channels, 1))
-    own = jnp.tile(jnp.repeat(eye, channels, axis=0), (1, group))
-    masked = lift_full * own
-    high = lax.reduce_precision(masked, 8, 7)
-    lh, ll = high.astype(BF16), (masked - high).astype(BF16)
-    lift_map = jnp.concatenate([lh, ll], 1)
     stored = spectral_weight.reshape(2 * modes, channels * channels)
 
     zc, zs = trig(np.arange(KZ), nz)
@@ -305,12 +319,6 @@
     yf = (yf * np.eye(a).reshape(1, 1, 1, a, 1, a, 1)).reshape(2 * rows * kyl * a, cols * cells).T
     yfh, yfl = np_halves(yf)
 
-    combined = jnp.dot(local_weight, lift_weight, precision=HIGHEST)
-    offset = jnp.dot(local_weight, lift_bias, precision=HIGHEST) + local_bias
-    origin = (lax.axis_index("row") == 0) & (lax.axis_index("col") == 0)
-    last = np.arange(group * channels)[None, :] >= width_in * channels
-    flag = jnp.where(jnp.asarray(last) & origin, 1.0, 0.0).astype(F32)
-
     results = []
     for sample in range(samples):
         vel = velocity[sample].reshape(width_in, cells, nz)
@@ -326,6 +334,7 @@
             in_specs=[vmem, vmem, smem, vmem, vmem, vmem, pl.BlockSpec(memory_space=pl.ANY)] + [vmem] * 8,
             out_specs=vmem,
             scratch_shapes=[
+                pltpu.VMEM((channels * channels, 2 * group * channels), BF16),
                 pltpu.VMEM(stored.shape, BF16),
                 pltpu.VMEM((2 * modes, group * channels), F32),
                 pltpu.VMEM((cols, width_in * rk, cells), F32),
@@ -346,8 +355,9 @@
                 vmem_limit_bytes=48 * 1024 * 1024, collective_id=0, has_side_effects=True
             ),
         )(
-            vel, tend, step, jnp.asarray(zf), jnp.asarray(yfh), jnp.asarray(yfl), stored, lift_map, jnp.asarray(xf),
-            jnp.asarray(selc, BF16), jnp.asarray(sels, BF16), flag, jnp.asarray(xb3), jnp.asarray(ybh), jnp.asarray(ybl),
+            vel, tend, step, jnp.asarray(zf), jnp.asarray(yfh), jnp.asarray(yfl), stored, lift_weight.T, lift_bias[None],
+            jnp.asarray(xf),
+            jnp.asarray(selc, BF16), jnp.asarray(sels, BF16), jnp.asarray(xb3), jnp.asarray(ybh), jnp.asarray(ybl),
         )
         pencils_z = pencils_z.reshape(cols * 2 * kzl * channels, cells)
         block = 4
@@ -358,13 +368,13 @@
             out_shape=jax.ShapeDtypeStruct((channels, cells, nz), BF16),
             in_specs=[
                 whole(*pencils_z.shape), whole(width_in, cells, nz), whole(width_in, cells, nz),
-                smem, smem, smem, whole(*zb3.shape),
+                smem, vmem, vmem, vmem, vmem, whole(*zb3.shape),
             ],
             out_specs=pl.BlockSpec((block, cells, nz), lambda i: (i, 0, 0)),
-            scratch_shapes=[pltpu.VMEM((width_in, cells, nz), F32)],
+            scratch_shapes=[pltpu.VMEM((width_in, cells, nz), F32), pltpu.VMEM((group, channels, nz), F32)],
             compiler_params=big,
         )(
-            pencils_z, vel, tend, step, combined, offset, jnp.asarray(zb3),
+            pencils_z, vel, tend, step, lift_weight.T, lift_bias[None], local_weight, local_bias[None], jnp.asarray(zb3),
         )
         results.append(features.reshape(channels, a, b, nz))
     return jnp.stack(results, 0)

time: 54.7 us -> 56.1 us (1.026)
  local copies, waits for them, and re-layouts: 5.5 us -> 11.7 us
  other arithmetic: 2.74 us -> 0 us
  matrix products: 1.61 us -> 0 us
  Pallas kernels: 43.5 us -> 42.9 us
    unnamed x26 -> x32, local copies, waits for them, and re-layouts: 0.07 us -> 11.7 us
    another operation x4 -> x0, local copies, waits for them, and re-layouts: 4.25 us -> none  [the longest x3 4.16 us: per_device(): own = jnp.tile(jnp.repeat(eye, channels, axis=0), (1, group))]
    dot_general x2 -> x0, matrix products: 1.61 us -> none  [the longest x1 0.81 us: per_device(): combined = jnp.dot(local_weight, lift_weight, precision=HIGHEST)]
    convert_element_type x2 -> x0, other arithmetic: 1.15 us -> none  [the longest x1 1.14 us: per_device(): lh, ll = (high.astype(BF16), (masked - high).astype(BF16))]
    broadcast_in_dim x2 -> x0, local copies, waits for them, and re-layouts: 1.09 us -> none  [the longest x1 1 us: per_device(): own = jnp.tile(jnp.repeat(eye, channels, axis=0), (1, group))]
    select_n x1 -> x0, other arithmetic: 0.81 us -> none  [per_device(): flag = jnp.where(jnp.asarray(last) & origin, 1.0, 0.0).astype(F32)]
    concatenate x2 -> x0, other arithmetic: 0.78 us -> none  [the longest x1 0.72 us: per_device(): lift4 = jnp.concatenate([lift_weight, lift_bias[:, None]], 1)]
    pallas_call x1, Pallas kernels: 6.21 us -> 5.64 us  [per_device(): pl.pallas_call(functools.partial(z_back_kernel, channels, block), grid=(c...]
where the time goes in v2:
time: 56.1 us; the launch traced here: 55.4 us
  Pallas kernels  42.9 us (76%)
  local copies, waits for them, and re-layouts  11.7 us (21%)
  between operations  0.71 us (1%)
    pallas_call x1, Pallas kernels, per_device(): pl.pallas_call(functools.partial(layer_kernel, kyl, kzl, part, 1.0 / (ful...  37.3 us
    unnamed x32, local copies, waits for them, and re-layouts  11.7 us
    pallas_call x1, Pallas kernels, per_device(): pl.pallas_call(functools.partial(z_back_kernel, channels, block), grid=(c...  5.64 us

profile of v2, /device:TPU:9, one launch (start us, length us, event | category | flops | bytes accessed | tf_op | source)
XLA Modules:
  0.0 55.4 jit_solution(14742715583280830635)
XLA Ops:
  0.7 0.0 copy-start
  0.7 1.0 %copy-done = f32[1,3,8,16,256]{4,3,2,1,0:T(8,128)S(1)} copy-done((f32[1,3,8,16,256]{4,3,2,1,0:T(8,128)S(1)}, f32[1,3,8,16,256]{4,3,2,1,0:T(8,128)}, u32[]{:S(2)}) %copy-start) | copy-done | bytes 393240
  1.6 0.0 copy-start.1
  1.7 1.0 %copy-done.1 = f32[1,3,8,16,256]{4,3,2,1,0:T(8,128)S(1)} copy-done((f32[1,3,8,16,256]{4,3,2,1,0:T(8,128)S(1)}, f32[1,3,8,16,256]{4,3,2,1,0:T(8,128)}, u32[]{:S(2)}) %copy-start.1) | copy-done | bytes 393240
  2.6 0.0 copy-start.2
  2.6 1.0 %copy-done.2 = bf16[128,2048]{1,0:T(8,128)(2,1)S(1)} copy-done((bf16[128,2048]{1,0:T(8,128)(2,1)S(1)}, bf16[128,2048]{1,0:T(8,128)(2,1)}, u32[]{:S(2)}) %copy-start.2) | copy-done | bytes 524312
  3.7 0.0 copy-start.3
  3.7 1.0 %copy-done.3 = bf16[128,2048]{1,0:T(8,128)(2,1)S(1)} copy-done((bf16[128,2048]{1,0:T(8,128)(2,1)S(1)}, bf16[128,2048]{1,0:T(8,128)(2,1)}, u32[]{:S(2)}) %copy-start.3) | copy-done | bytes 524312
  4.7 0.0 copy-start.4
  4.7 1.0 %copy-done.4 = bf16[512,512]{1,0:T(8,128)(2,1)S(1)} copy-done((bf16[512,512]{1,0:T(8,128)(2,1)S(1)}, bf16[512,512]{1,0:T(8,128)(2,1)}, u32[]{:S(2)}) %copy-start.4) | copy-done | bytes 524312
  5.8 0.0 copy-start.5
  5.8 1.0 %copy-done.5 = bf16[512,512]{1,0:T(8,128)(2,1)S(1)} copy-done((bf16[512,512]{1,0:T(8,128)(2,1)S(1)}, bf16[512,512]{1,0:T(8,128)(2,1)}, u32[]{:S(2)}) %copy-start.5) | copy-done | bytes 524312
  6.8 0.0 copy-start.6
  6.8 0.9 %copy-done.6 = bf16[4,4,16,256]{3,2,1,0:T(8,128)(2,1)S(1)} copy-done((bf16[4,4,16,256]{3,2,1,0:T(8,128)(2,1)S(1)}, bf16[4,4,16,256]{3,2,1,0:T(8,128)(2,1)}, u32[]{:S(2)}) %copy-start.6) | copy-done | bytes 131096
  7.7 0.0 copy-start.7
  7.7 0.9 %copy-done.7 = bf16[4,4,16,256]{3,2,1,0:T(8,128)(2,1)S(1)} copy-done((bf16[4,4,16,256]{3,2,1,0:T(8,128)(2,1)S(1)}, bf16[4,4,16,256]{3,2,1,0:T(8,128)(2,1)}, u32[]{:S(2)}) %copy-start.7) | copy-done | bytes 131096
  8.6 0.0 copy-start.9
  8.6 0.8 %copy-done.9 = bf16[128,192]{1,0:T(8,128)(2,1)S(1)} copy-done((bf16[128,192]{1,0:T(8,128)(2,1)S(1)}, bf16[128,192]{1,0:T(8,128)(2,1)}, u32[]{:S(2)}) %copy-start.9) | copy-done | bytes 49176
  9.5 0.0 copy-start.10
  9.5 0.8 %copy-done.10 = f32[64,256]{1,0:T(8,128)S(1)} copy-done((f32[64,256]{1,0:T(8,128)S(1)}, f32[64,256]{1,0:T(8,128)}, u32[]{:S(2)}) %copy-start.10) | copy-done | bytes 65560
  10.3 0.0 copy-start.11
  10.3 0.8 %copy-done.11 = f32[64,64]{1,0:T(8,128)S(1)} copy-done((f32[64,64]{1,0:T(8,128)S(1)}, f32[64,64]{1,0:T(8,128)}, u32[]{:S(2)}) %copy-start.11) | copy-done | bytes 16408
  11.1 0.0 copy-start.13
  11.1 0.7 %copy-done.13 = f32[32,3]{0,1:T(4,128)S(1)} copy-done((f32[32,3]{0,1:T(4,128)S(1)}, f32[32,3]{0,1:T(4,128)}, u32[]{:S(2)}) %copy-start.13) | copy-done | bytes 408
  11.7 0.0 copy-start.14
  11.7 0.7 %copy-done.14 = f32[32]{0:T(128)S(1)} copy-done((f32[32]{0:T(128)S(1)}, f32[32]{0:T(128)}, u32[]{:S(2)}) %copy-start.14) | copy-done | bytes 152
  12.4 0.0 copy-start.8
  12.4 0.0 copy-start.12
  12.4 0.0 copy-start.15
  12.4 37.3 %shard_map.172 = f32[4,2,256,128]{3,2,1,0:T(8,128)S(1)} custom-call(f32[3,128,256]{2,1,0:T(8,128)S(1)} %bitcast.9, f32[3,128,256]{2,1,0:T(8,128)S(1)} %bitcast.11, f32[1]{0:T(128)S(6)} %copy.19.step_ref, f32[64,256]{1,0:T(8,128)S(1)} %copy-done.10, bf16[512,512]{1,0:T(8,128)(2,1)S(1)} %copy-done.5, bf16[512,512]{1,0:T(8,128)(2,1)S(1)} %copy-done.4, ...), custom_call_target="tpu_custom_call" | custom-call | tf_op jit(solution)/shard_map/pallas_call | solution.py:331
  49.7 0.0 copy-done.8
  49.7 0.0 copy-done.12
  49.7 0.0 copy-done.15
  49.7 5.6 %shard_map.173 = bf16[32,128,256]{2,1,0:T(8,128)(2,1)} custom-call(f32[2048,128]{1,0:T(8,128)S(1)} %bitcast.8, f32[3,128,256]{2,1,0:T(8,128)S(1)} %bitcast.10, f32[3,128,256]{2,1,0:T(8,128)S(1)} %bitcast.12, f32[1]{0:T(128)S(6)} %copy.19.step_ref, f32[3,32]{1,0:T(4,128)S(1)} %bitcast.14, f32[1,32]{1,0:T(1,128)S(1)} %bitcast.16, f32[32,32]{1,0:T(8,128)S(1)} %copy-done.12, ...), custom_call_target="tpu_custom_call" | custom-call | tf_op jit(solution)/shard_map/pallas_call | solution.py:365
Async XLA Ops:
  0.7 1.0 %copy-start = (f32[1,3,8,16,256]{4,3,2,1,0:T(8,128)S(1)}, f32[1,3,8,16,256]{4,3,2,1,0:T(8,128)}, u32[]{:S(2)}) copy-start(f32[1,3,8,16,256]{4,3,2,1,0:T(8,128)} %param.18) | copy-start | bytes 1179652
  1.6 1.0 %copy-start.1 = (f32[1,3,8,16,256]{4,3,2,1,0:T(8,128)S(1)}, f32[1,3,8,16,256]{4,3,2,1,0:T(8,128)}, u32[]{:S(2)}) copy-start(f32[1,3,8,16,256]{4,3,2,1,0:T(8,128)} %param.19) | copy-start | bytes 1179652
  2.6 1.0 %copy-start.2 = (bf16[128,2048]{1,0:T(8,128)(2,1)S(1)}, bf16[128,2048]{1,0:T(8,128)(2,1)}, u32[]{:S(2)}) copy-start(bf16[128,2048]{1,0:T(8,128)(2,1)} %constant.25.clone.sels_ref) | copy-start | bytes 1572868
  3.7 1.0 %copy-start.3 = (bf16[128,2048]{1,0:T(8,128)(2,1)S(1)}, bf16[128,2048]{1,0:T(8,128)(2,1)}, u32[]{:S(2)}) copy-start(bf16[128,2048]{1,0:T(8,128)(2,1)} %constant.24.clone.selc_ref) | copy-start | bytes 1572868
  4.7 1.0 %copy-start.4 = (bf16[512,512]{1,0:T(8,128)(2,1)S(1)}, bf16[512,512]{1,0:T(8,128)(2,1)}, u32[]{:S(2)}) copy-start(bf16[512,512]{1,0:T(8,128)(2,1)} %constant.22.clone.yfl_ref) | copy-start | bytes 1572868
  5.8 1.0 %copy-start.5 = (bf16[512,512]{1,0:T(8,128)(2,1)S(1)}, bf16[512,512]{1,0:T(8,128)(2,1)}, u32[]{:S(2)}) copy-start(bf16[512,512]{1,0:T(8,128)(2,1)} %constant.21.clone.yfh_ref) | copy-start | bytes 1572868
  6.8 0.9 %copy-start.6 = (bf16[4,4,16,256]{3,2,1,0:T(8,128)(2,1)S(1)}, bf16[4,4,16,256]{3,2,1,0:T(8,128)(2,1)}, u32[]{:S(2)}) copy-start(bf16[4,4,16,256]{3,2,1,0:T(8,128)(2,1)} %constant.28.clone.yl_ref) | copy-start | bytes 393220
  7.7 0.9 %copy-start.7 = (bf16[4,4,16,256]{3,2,1,0:T(8,128)(2,1)S(1)}, bf16[4,4,16,256]{3,2,1,0:T(8,128)(2,1)}, u32[]{:S(2)}) copy-start(bf16[4,4,16,256]{3,2,1,0:T(8,128)(2,1)} %constant.27.clone.yh_ref) | copy-start | bytes 393220
  8.6 0.8 %copy-start.9 = (bf16[128,192]{1,0:T(8,128)(2,1)S(1)}, bf16[128,192]{1,0:T(8,128)(2,1)}, u32[]{:S(2)}) copy-start(bf16[128,192]{1,0:T(8,128)(2,1)} %constant.26.clone.xb_ref) | copy-start | bytes 147460
  9.5 0.8 %copy-start.10 = (f32[64,256]{1,0:T(8,128)S(1)}, f32[64,256]{1,0:T(8,128)}, u32[]{:S(2)}) copy-start(f32[64,256]{1,0:T(8,128)} %constant.20.clone.zf_ref) | copy-start | bytes 196612
  10.3 0.8 %copy-start.11 = (f32[64,64]{1,0:T(8,128)S(1)}, f32[64,64]{1,0:T(8,128)}, u32[]{:S(2)}) copy-start(f32[64,64]{1,0:T(8,128)} %constant.23.clone.xf_ref) | copy-start | bytes 49156
  11.1 0.7 %copy-start.13 = (f32[32,3]{0,1:T(4,128)S(1)}, f32[32,3]{0,1:T(4,128)}, u32[]{:S(2)}) copy-start(f32[32,3]{0,1:T(4,128)} %param.21) | copy-start | bytes 1156
  11.7 0.7 %copy-start.14 = (f32[32]{0:T(128)S(1)}, f32[32]{0:T(128)}, u32[]{:S(2)}) copy-start(f32[32]{0:T(128)} %param.22) | copy-start | bytes 388
  12.4 37.3 %copy-start.8 = (bf16[192,256]{1,0:T(8,128)(2,1)S(1)}, bf16[192,256]{1,0:T(8,128)(2,1)}, u32[]{:S(2)}) copy-start(bf16[192,256]{1,0:T(8,128)(2,1)} %constant.29.clone.tz_ref) | copy-start | bytes 294916
  12.4 37.3 %copy-start.12 = (f32[32,32]{1,0:T(8,128)S(1)}, f32[32,32]{1,0:T(8,128)}, u32[]{:S(2)}) copy-start(f32[32,32]{1,0:T(8,128)} %mw_ref.1) | copy-start | bytes 12292
  12.4 37.3 %copy-start.15 = (f32[32]{0:T(128)S(1)}, f32[32]{0:T(128)}, u32[]{:S(2)}) copy-start(f32[32]{0:T(128)} %param.25) | copy-start | bytes 388
